TPU v7x, 32 devices: a whole 2x2x4 slice. The times are simulated.
32 devices in a mesh: grp: 2 (over x), band: 16 (over z, y, core).
Axes of the slice: x: 2, y: 2, z: 4, core: 2. Of those that a mesh axis runs over, the one named last changes fastest.
Arguments:
- source: bfloat16 [262144, 640], P(('grp', 'band')), parts along dimension 0, may hold values from -96 to 96
- tiles: bfloat16 [4096, 128, 128], P('band'), may hold values from 0 to 0.001953125
- tile_slot: int32 [4096], P('band'), may hold values from 0 to 31, as said below
- tile_dst: int32 [4096], P('band'), may hold values from 0 to 31
- send_index: int32 [16, 32], P('band'), may hold values from 0 to 63
- send_count: int32 [16, 16], P('band'), may hold values from 1 to 2, as said below
- polar_tiles: bfloat16 [1024, 128, 128], P('band'), may hold values from 0 to 0.00024414062
- polar_src: int32 [1024], P('band'), may hold values from 0 to 63
- polar_dst: int32 [1024], P('band'), may hold values from 0 to 15
Outputs:
- model_field: bfloat16 [131072, 640], P(('grp', 'band')), parts along dimension 0
- polar_cap: bfloat16 [4096, 640], P(('grp', 'band')), parts along dimension 0
There are 2 independent parts, one for each index of `grp`. A program takes and returns all parts, laid end to end along the dimension named above; an argument that names none is the same for every part. Nothing has to cross between parts.
Inputs may be any that keep to these rules, and one draw needn't show every extreme that they name: `send_count`: entry [s, o] counts the used slots of band s for owner o; every row has an entry 2, and some owner has 2 from every band. `tile_slot`: tile t names slot s * 2 + j of owner t // 256 with j below send_count[s, t // 256]; every used slot is named by some tile of its owner.
All inputs are finite; a program needn't handle non-finite values.
Results may differ from a plain program's by a relative error of at most 0.001.
Values may be sent and summed in bfloat16 or wider, within the bound.
A program may use at most 192 MiB of HBM per device.

v0:
```python
import jax
import jax.numpy as jnp
from jax import lax
from jax.sharding import PartitionSpec as P

PB_DEV = 1
TB_DEV = 32


def on_device(
    source, tiles, tile_slot, tile_dst, send_index, send_count, polar_tiles, polar_src, polar_dst
):
    owners = lax.axis_size("band")
    width = tiles.shape[1]
    feats = source.shape[1]
    per_owner = send_index.shape[1] // owners
    blocks = source.reshape(-1, width, feats)
    polar_inputs = blocks[polar_src]
    polar_terms = jnp.einsum(
        "tps,tsf->tpf", polar_tiles, polar_inputs, preferred_element_type=jnp.float32
    )
    cap_part = (
        jnp.zeros((PB_DEV * owners, width, feats), jnp.float32).at[polar_dst].add(polar_terms)
    )
    usable = lax.broadcasted_iota(jnp.int32, (owners, per_owner), 1) < send_count[0][:, None]
    outgoing = blocks[send_index[0]]
    outgoing = jnp.where(usable.reshape(-1)[:, None, None], outgoing, jnp.zeros((), jnp.bfloat16))
    received = lax.all_to_all(
        outgoing.reshape(owners, per_owner, width, feats),
        "band",
        split_axis=0,
        concat_axis=0,
        tiled=True,
    )
    arrived = received.reshape(owners * per_owner, width, feats)
    group = 32
    turns = tiles.shape[0] // group

    def accumulate(total, items):
        weights, slots, places = items
        inputs = arrived[slots]
        products = jnp.einsum("tps,tsf->tpf", weights, inputs, preferred_element_type=jnp.float32)
        return (total.at[places].add(products), None)

    field, _ = lax.scan(
        accumulate,
        jnp.zeros((TB_DEV, width, feats), jnp.float32),
        (
            tiles.reshape(turns, group, width, width),
            tile_slot.reshape(turns, group),
            tile_dst.reshape(turns, group),
        ),
    )
    rounded = field.astype(jnp.bfloat16).reshape(TB_DEV // owners, owners, width, feats)
    placed = lax.all_to_all(rounded, "band", split_axis=1, concat_axis=0, tiled=True)
    model_field = placed.reshape(TB_DEV * width, feats)
    own_cap = lax.psum_scatter(cap_part, "band", scatter_dimension=0, tiled=True)
    polar_cap = own_cap.reshape(PB_DEV * width, feats).astype(jnp.bfloat16)
    return (model_field, polar_cap)


def solution(mesh):
    placed = (
        P(("grp", "band"), None),
        P("band", None, None),
        P("band"),
        P("band"),
        P("band", None),
        P("band", None),
        P("band", None, None),
        P("band"),
        P("band"),
    )
    return jax.shard_map(
        on_device,
        mesh=mesh,
        in_specs=placed,
        out_specs=(P(("grp", "band"), None), P(("grp", "band"), None)),
        check_vma=False,
    )
```

profile of v0, /device:TPU:13, one launch (start us, length us, event | category | flops | bytes accessed | tf_op | source)
XLA Modules:
  0.0 626.4 jit_solution(13259404906195864424)
XLA Ops:
  8.7 7.5 %gather_fusion.1 = bf16[32,128,640]{2,1,0:T(8,128)(2,1)} fusion(bf16[64,128,640]{2,1,0:T(8,128)(2,1)} %bitcast.49, s32[1024]{0:T(1024)S(1)} %pad_clamp_fusion.2), kind=kCustom, calls=%fused_computation.1 | custom fusion | bytes 10485888 | tf_op jit(solution)/shard_map/gather | solution.py:26
  28.3 114.8 %all-to-all-done = bf16[16,2,128,640]{3,2,1,0:T(8,128)(2,1)} async-done(((bf16[16,2,128,640]{3,2,1,0:T(8,128)(2,1)}), bf16[16,2,128,640]{3,2,1,0:T(8,128)(2,1)}, u32[]{:S(2)}, u32[]{:S(2)}) %all-to-all-start) | async-done | bytes 5242912 | tf_op jit(solution)/shard_map/all_to_all | solution.py:28
  148.1 284.8 %while.10 = (s32[]{:T(128)}, f32[32,128,640]{2,1,0:T(8,128)}, s32[8,32]{1,0:T(8,128)S(1)}, bf16[8,32,128,128]{3,2,1,0:T(8,128)(2,1)}, s32[8,32]{1,0:T(8,128)S(1)}, /*index=5*/bf16[32,128,640]{2,1,0:T(8,128)(2,1)}, s32[]{:T(128)}) while((s32[]{:T(128)}, f32[32,128,640]{2,1,0:T(8,128)}, s32[8,32]{1,0:T(8,128)S(1)}, ...), condition=%wide.region_2.3_spmd, body=%wide.region_0.2_spmd.sunk | while | flops 673711296 | bytes 58725840 | solution.py:45
  154.2 8.3 %fusion.19 = f32[32,128,640]{2,1,0:T(8,128)} fusion(bf16[32,128,640]{2,1,0:T(8,128)(2,1)} %gather_fusion, bf16[8,32,128,128]{3,2,1,0:T(8,128)(2,1)} %get-tuple-element.107, s32[]{:T(128)} %get-tuple-element.97), kind=kOutput, calls=%fused_computation.5.clone.1 | convolution fusion | flops 671088640 | bytes 16777728 | tf_op jit(solution)/shard_map/while/body/eval_jaxpr/tps,tsf->tpf/dot_general | solution.py:42
  162.5 21.2 %scatter_fusion = f32[32,128,640]{2,1,0:T(8,128)} fusion(f32[32,128,640]{2,1,0:T(8,128)} %get-tuple-element.98, s32[32]{0:T(128)S(1)} %get-tuple-element.88, f32[32,128,640]{2,1,0:T(8,128)} %fusion.19), kind=kCustom, calls=%fused_computation.3.clone.1 | custom fusion | flops 2621440 | bytes 31457408 | tf_op jit(solution)/shard_map/while/body/eval_jaxpr/scatter-add | solution.py:43
  189.8 8.3 %fusion.19 = f32[32,128,640]{2,1,0:T(8,128)} fusion(bf16[32,128,640]{2,1,0:T(8,128)(2,1)} %gather_fusion, bf16[8,32,128,128]{3,2,1,0:T(8,128)(2,1)} %get-tuple-element.107, s32[]{:T(128)} %get-tuple-element.97), kind=kOutput, calls=%fused_computation.5.clone.1 | convolution fusion | flops 671088640 | bytes 16777728 | tf_op jit(solution)/shard_map/while/body/eval_jaxpr/tps,tsf->tpf/dot_general | solution.py:42
  198.1 21.0 %scatter_fusion = f32[32,128,640]{2,1,0:T(8,128)} fusion(f32[32,128,640]{2,1,0:T(8,128)} %get-tuple-element.98, s32[32]{0:T(128)S(1)} %get-tuple-element.88, f32[32,128,640]{2,1,0:T(8,128)} %fusion.19), kind=kCustom, calls=%fused_computation.3.clone.1 | custom fusion | flops 2621440 | bytes 31457408 | tf_op jit(solution)/shard_map/while/body/eval_jaxpr/scatter-add | solution.py:43
  225.2 8.3 %fusion.19 = f32[32,128,640]{2,1,0:T(8,128)} fusion(bf16[32,128,640]{2,1,0:T(8,128)(2,1)} %gather_fusion, bf16[8,32,128,128]{3,2,1,0:T(8,128)(2,1)} %get-tuple-element.107, s32[]{:T(128)} %get-tuple-element.97), kind=kOutput, calls=%fused_computation.5.clone.1 | convolution fusion | flops 671088640 | bytes 16777728 | tf_op jit(solution)/shard_map/while/body/eval_jaxpr/tps,tsf->tpf/dot_general | solution.py:42
  233.5 21.2 %scatter_fusion = f32[32,128,640]{2,1,0:T(8,128)} fusion(f32[32,128,640]{2,1,0:T(8,128)} %get-tuple-element.98, s32[32]{0:T(128)S(1)} %get-tuple-element.88, f32[32,128,640]{2,1,0:T(8,128)} %fusion.19), kind=kCustom, calls=%fused_computation.3.clone.1 | custom fusion | flops 2621440 | bytes 31457408 | tf_op jit(solution)/shard_map/while/body/eval_jaxpr/scatter-add | solution.py:43
  260.8 8.3 %fusion.19 = f32[32,128,640]{2,1,0:T(8,128)} fusion(bf16[32,128,640]{2,1,0:T(8,128)(2,1)} %gather_fusion, bf16[8,32,128,128]{3,2,1,0:T(8,128)(2,1)} %get-tuple-element.107, s32[]{:T(128)} %get-tuple-element.97), kind=kOutput, calls=%fused_computation.5.clone.1 | convolution fusion | flops 671088640 | bytes 16777728 | tf_op jit(solution)/shard_map/while/body/eval_jaxpr/tps,tsf->tpf/dot_general | solution.py:42
  269.1 21.3 %scatter_fusion = f32[32,128,640]{2,1,0:T(8,128)} fusion(f32[32,128,640]{2,1,0:T(8,128)} %get-tuple-element.98, s32[32]{0:T(128)S(1)} %get-tuple-element.88, f32[32,128,640]{2,1,0:T(8,128)} %fusion.19), kind=kCustom, calls=%fused_computation.3.clone.1 | custom fusion | flops 2621440 | bytes 31457408 | tf_op jit(solution)/shard_map/while/body/eval_jaxpr/scatter-add | solution.py:43
  296.5 8.3 %fusion.19 = f32[32,128,640]{2,1,0:T(8,128)} fusion(bf16[32,128,640]{2,1,0:T(8,128)(2,1)} %gather_fusion, bf16[8,32,128,128]{3,2,1,0:T(8,128)(2,1)} %get-tuple-element.107, s32[]{:T(128)} %get-tuple-element.97), kind=kOutput, calls=%fused_computation.5.clone.1 | convolution fusion | flops 671088640 | bytes 16777728 | tf_op jit(solution)/shard_map/while/body/eval_jaxpr/tps,tsf->tpf/dot_general | solution.py:42
  304.8 21.4 %scatter_fusion = f32[32,128,640]{2,1,0:T(8,128)} fusion(f32[32,128,640]{2,1,0:T(8,128)} %get-tuple-element.98, s32[32]{0:T(128)S(1)} %get-tuple-element.88, f32[32,128,640]{2,1,0:T(8,128)} %fusion.19), kind=kCustom, calls=%fused_computation.3.clone.1 | custom fusion | flops 2621440 | bytes 31457408 | tf_op jit(solution)/shard_map/while/body/eval_jaxpr/scatter-add | solution.py:43
  332.2 8.3 %fusion.19 = f32[32,128,640]{2,1,0:T(8,128)} fusion(bf16[32,128,640]{2,1,0:T(8,128)(2,1)} %gather_fusion, bf16[8,32,128,128]{3,2,1,0:T(8,128)(2,1)} %get-tuple-element.107, s32[]{:T(128)} %get-tuple-element.97), kind=kOutput, calls=%fused_computation.5.clone.1 | convolution fusion | flops 671088640 | bytes 16777728 | tf_op jit(solution)/shard_map/while/body/eval_jaxpr/tps,tsf->tpf/dot_general | solution.py:42
  340.5 21.3 %scatter_fusion = f32[32,128,640]{2,1,0:T(8,128)} fusion(f32[32,128,640]{2,1,0:T(8,128)} %get-tuple-element.98, s32[32]{0:T(128)S(1)} %get-tuple-element.88, f32[32,128,640]{2,1,0:T(8,128)} %fusion.19), kind=kCustom, calls=%fused_computation.3.clone.1 | custom fusion | flops 2621440 | bytes 31457408 | tf_op jit(solution)/shard_map/while/body/eval_jaxpr/scatter-add | solution.py:43
  367.9 8.3 %fusion.19 = f32[32,128,640]{2,1,0:T(8,128)} fusion(bf16[32,128,640]{2,1,0:T(8,128)(2,1)} %gather_fusion, bf16[8,32,128,128]{3,2,1,0:T(8,128)(2,1)} %get-tuple-element.107, s32[]{:T(128)} %get-tuple-element.97), kind=kOutput, calls=%fused_computation.5.clone.1 | convolution fusion | flops 671088640 | bytes 16777728 | tf_op jit(solution)/shard_map/while/body/eval_jaxpr/tps,tsf->tpf/dot_general | solution.py:42
  376.2 20.9 %scatter_fusion = f32[32,128,640]{2,1,0:T(8,128)} fusion(f32[32,128,640]{2,1,0:T(8,128)} %get-tuple-element.98, s32[32]{0:T(128)S(1)} %get-tuple-element.88, f32[32,128,640]{2,1,0:T(8,128)} %fusion.19), kind=kCustom, calls=%fused_computation.3.clone.1 | custom fusion | flops 2621440 | bytes 31457408 | tf_op jit(solution)/shard_map/while/body/eval_jaxpr/scatter-add | solution.py:43
  403.1 8.3 %fusion.19 = f32[32,128,640]{2,1,0:T(8,128)} fusion(bf16[32,128,640]{2,1,0:T(8,128)(2,1)} %gather_fusion, bf16[8,32,128,128]{3,2,1,0:T(8,128)(2,1)} %get-tuple-element.107, s32[]{:T(128)} %get-tuple-element.97), kind=kOutput, calls=%fused_computation.5.clone.1 | convolution fusion | flops 671088640 | bytes 16777728 | tf_op jit(solution)/shard_map/while/body/eval_jaxpr/tps,tsf->tpf/dot_general | solution.py:42
  411.5 21.5 %scatter_fusion = f32[32,128,640]{2,1,0:T(8,128)} fusion(f32[32,128,640]{2,1,0:T(8,128)} %get-tuple-element.98, s32[32]{0:T(128)S(1)} %get-tuple-element.88, f32[32,128,640]{2,1,0:T(8,128)} %fusion.19), kind=kCustom, calls=%fused_computation.3.clone.1 | custom fusion | flops 2621440 | bytes 31457408 | tf_op jit(solution)/shard_map/while/body/eval_jaxpr/scatter-add | solution.py:43
  446.8 10.7 %gather_fusion.2 = bf16[64,128,640]{2,1,0:T(8,128)(2,1)} fusion(bf16[64,128,640]{2,1,0:T(8,128)(2,1)} %bitcast.50, s32[1024]{0:T(1024)S(1)} %pad_clamp_fusion.1), kind=kCustom, calls=%fused_computation.2 | custom fusion | bytes 20971776 | tf_op jit(solution)/shard_map/gather | solution.py:18
  457.5 11.0 %convolution_bitcast_fusion = f32[64,128,640]{1,2,0:T(8,128)} fusion(bf16[64,128,640]{2,1,0:T(8,128)(2,1)} %gather_fusion.2, bf16[64,128,128]{2,1,0:T(8,128)(2,1)S(1)} %copy-done), kind=kOutput, calls=%fused_computation.18 | convolution fusion | flops 1342177280 | bytes 33554432 | tf_op jit(solution)/shard_map/tps,tsf->tpf/dot_general | solution.py:19
  468.5 22.8 %copy.15 = f32[64,128,640]{2,1,0:T(8,128)} copy(f32[64,128,640]{1,2,0:T(8,128)} %convolution_bitcast_fusion) | data formatting | bytes 41943040 | tf_op jit(solution)/shard_map/tps,tsf->tpf/dot_general | solution.py:19
  494.2 41.9 %scatter_fusion.1 = f32[16,128,640]{2,1,0:T(8,128)} fusion(f32[16,128,640]{2,1,0:T(8,128)} %broadcast_in_dim.30, s32[64]{0:T(128)S(1)} %compare_select_fusion.3, f32[64,128,640]{2,1,0:T(8,128)} %copy.15), kind=kCustom, calls=%fused_computation.4 | custom fusion | flops 5242880 | bytes 62914816 | tf_op jit(solution)/shard_map/scatter-add | solution.py:23
  536.1 76.5 %reduce-scatter.2.cloned.1.call-done = f32[1,128,640]{2,1,0:T(8,128)} async-done(((f32[16,128,640]{2,1,0:T(8,128)}), f32[1,128,640]{2,1,0:T(8,128)}) %reduce-scatter.2.cloned.1.call-update) | async-done | bytes 327696 | tf_op jit(solution)/shard_map/reduce_scatter | solution.py:57
  (54 shorter events, 90.7 us)
Async XLA Ops:
  7.2 450.3 %copy-start = (bf16[64,128,128]{2,1,0:T(8,128)(2,1)S(1)}, bf16[64,128,128]{2,1,0:T(8,128)(2,1)}, u32[]{:S(2)}) copy-start(bf16[64,128,128]{2,1,0:T(8,128)(2,1)} %param.17) | copy-start | bytes 6291460
  16.2 11.9 %copy-start.1 = (s32[256]{0:T(256)S(1)}, s32[256]{0:T(256)}, u32[]{:S(2)}) copy-start(s32[256]{0:T(256)} %param.14) | copy-start | bytes 3076
  16.2 12.0 %copy-start.2 = (s32[256]{0:T(256)S(1)}, s32[256]{0:T(256)}, u32[]{:S(2)}) copy-start(s32[256]{0:T(256)} %param.13) | copy-start | bytes 3076
  21.6 121.5 %all-to-all-start = ((bf16[16,2,128,640]{3,2,1,0:T(8,128)(2,1)}), bf16[16,2,128,640]{3,2,1,0:T(8,128)(2,1)}, u32[]{:S(2)}, u32[]{:S(2)}) async-start(bf16[16,2,128,640]{3,2,1,0:T(8,128)(2,1)} %broadcast_select_fusion), calls=%async_computation | async-start | bytes 10485760 | tf_op jit(solution)/shard_map/all_to_all | solution.py:28
  437.7 9.1 %copy-start.3 = (s32[64]{0:T(128)S(1)}, s32[64]{0:T(128)}, u32[]{:S(2)}) copy-start(s32[64]{0:T(128)} %param.18) | copy-start | bytes 772
  440.5 173.7 %all-to-all-start.1 = ((bf16[2,16,128,640]{3,2,0,1:T(8,128)(2,1)}), bf16[2,16,128,640]{3,2,0,1:T(8,128)(2,1)}, u32[]{:S(2)}, u32[]{:S(2)}) async-start(bf16[2,16,128,640]{3,2,0,1:T(8,128)(2,1)} %copy.13), calls=%async_computation.1 | async-start | bytes 10485760 | tf_op jit(solution)/shard_map/all_to_all | solution.py:55
  446.5 166.1 %reduce-scatter.2.cloned.1.call-start = ((), (), s32[]{:S(2)}) async-start(), calls=%async_computation.3 | async-start | bytes 5570560 | tf_op jit(solution)/shard_map/reduce_scatter | solution.py:57
  468.5 22.8 %copy-start.4 = (s32[64]{0:T(128)S(1)}, s32[64]{0:T(128)}, u32[]{:S(2)}) copy-start(s32[64]{0:T(128)} %param.19) | copy-start | bytes 772
Sparse Core Ops, SparseCore 0:
  536.2 76.3 reduce-scatter.1
where the time goes:
time: 632 us; the launch traced here: 626 us
  other arithmetic  225 us (36%)
  waiting for transfers between devices  191 us (30%)
  local copies, waits for them, and re-layouts  105 us (17%)
  matrix products  77.5 us (12%)
  between operations  14.1 us (2%)
  starting transfers between devices  12.8 us (2%)
    scatter-add x8, other arithmetic, accumulate(): return (total.at[places].add(products), None)  170 us
    all_to_all x1, waiting for transfers between devices, on_device(): lax.all_to_all(outgoing.reshape(owners, per_owner, width, feats), 'band',...  115 us
    reduce_scatter x1, waiting for transfers between devices, on_device(): lax.psum_scatter(cap_part, 'band', scatter_dimension=0, tiled=True)  76.5 us
    dot_general x8, matrix products, accumulate(): jnp.einsum('tps,tsf->tpf', weights, inputs, preferred_element_type=jnp.fl...  66.5 us
    gather x8, local copies, waits for them, and re-layouts, accumulate(): inputs = arrived[slots]  48.2 us
    scatter-add x1, other arithmetic, on_device(): jnp.zeros((PB_DEV * owners, width, feats), jnp.float32).at[polar_dst]  41.9 us
    dot_general x1, local copies, waits for them, and re-layouts, on_device(): jnp.einsum('tps,tsf->tpf', polar_tiles, polar_inputs, preferred_element_t...  22.8 us
  transfers between devices with their start and end apart: 3, of which 2 were waited for; matrix products, arithmetic and copies ran while one was open for 15% of the time, Pallas kernels for 0%

commit v1 on v0

v1 whole, which is shorter than its diff:
```python
import functools

import jax
import jax.numpy as jnp
from jax import lax
from jax.experimental import pallas as pl
from jax.experimental.pallas import tpu as pltpu
from jax.sharding import PartitionSpec as P

PB_DEV = 1
TB_DEV = 32
GROUP = 4


def plan(dst, slot, blocks):
    count = dst.shape[0]
    groups = count // GROUP + blocks
    same = dst[:, None] == dst[None, :]
    earlier = jnp.arange(count)[:, None] > jnp.arange(count)[None, :]
    rank = jnp.sum(same & earlier, axis=1, dtype=jnp.int32)
    held = jnp.sum(
        dst[None, :] == jnp.arange(blocks, dtype=jnp.int32)[:, None], axis=1, dtype=jnp.int32
    )
    need = (held + GROUP - 1) // GROUP
    ids = jnp.arange(blocks)
    ends = jnp.sum(jnp.where(ids[:, None] >= ids[None, :], need[None, :], 0), axis=1)
    first = ends - need
    start = jnp.sum(
        jnp.where(dst[:, None] == ids[None, :], first[None, :], 0), axis=1, dtype=jnp.int32
    )
    place = start * GROUP + rank
    hit = place[None, :] == jnp.arange(groups * GROUP, dtype=jnp.int32)[:, None]
    tile_at = jnp.sum(
        jnp.where(hit, jnp.arange(1, count + 1, dtype=jnp.int32)[None, :], 0), axis=1
    )
    slot_at = jnp.sum(jnp.where(hit, slot[None, :], 0), axis=1)
    g = jnp.arange(groups, dtype=jnp.int32)
    dst_at = jnp.sum(ends[None, :] <= g[:, None], axis=1, dtype=jnp.int32)
    return tile_at, slot_at, dst_at, ends[-1:]


def block_kernel(tile_at, slot_at, dst_at, total, tiles, inputs, out, acc):
    acc[...] = jnp.zeros_like(acc)

    def step(g, carry):
        weights = []
        values = []
        for i in range(GROUP):
            t = tile_at[g * GROUP + i]
            w = tiles[jnp.maximum(t - 1, 0)]
            weights.append(jnp.where(t > 0, w, jnp.zeros_like(w)))
            values.append(inputs[slot_at[g * GROUP + i]])
        d = dst_at[g]
        acc[d] += jnp.dot(
            jnp.concatenate(weights, axis=1),
            jnp.concatenate(values, axis=0),
            preferred_element_type=jnp.float32,
        )
        return carry

    lax.fori_loop(0, total[0], step, 0)
    if out is not acc:
        out[...] = acc[...].astype(out.dtype)


def cap_kernel(tile_at, slot_at, dst_at, total, tiles, inputs, out):
    block_kernel(tile_at, slot_at, dst_at, total, tiles, inputs, out, out)


def block_matmul(tables, tiles, inputs, blocks, dtype, name):
    count, width, _ = tiles.shape
    feats = inputs.shape[2]
    rounds = dtype != jnp.float32
    return pl.pallas_call(
        block_kernel if rounds else cap_kernel,
        out_shape=jax.ShapeDtypeStruct((blocks, width, feats), dtype),
        in_specs=[pl.BlockSpec(memory_space=pltpu.SMEM)] * 4
        + [pl.BlockSpec(memory_space=pltpu.VMEM)] * 2,
        out_specs=pl.BlockSpec(memory_space=pltpu.VMEM),
        scratch_shapes=[pltpu.VMEM((blocks, width, feats), jnp.float32)] if rounds else [],
        compiler_params=pltpu.CompilerParams(vmem_limit_bytes=56 * 1024 * 1024),
        cost_estimate=pl.CostEstimate(
            flops=4 * count * width * width * feats,
            bytes_accessed=2 * (tiles.size + inputs.size) + 4 * blocks * width * feats,
            transcendentals=0,
        ),
        name=name,
    )(*tables, tiles, inputs)


def gather_kernel(index, blocks, out, held, in_sem, out_sem):
    count = out.shape[0]
    reads = [
        pltpu.make_async_copy(blocks.at[index[0, i]], held.at[i], in_sem.at[i])
        for i in range(count)
    ]
    writes = [
        pltpu.make_async_copy(held.at[i], out.at[i], out_sem.at[i]) for i in range(count)
    ]
    for copy in reads:
        copy.start()
    for read, write in zip(reads, writes):
        read.wait()
        write.start()
    for copy in writes:
        copy.wait()


def gather_blocks(index, blocks):
    count = index.shape[1]
    shape = (count,) + blocks.shape[1:]
    return pl.pallas_call(
        gather_kernel,
        out_shape=jax.ShapeDtypeStruct(shape, blocks.dtype),
        in_specs=[
            pl.BlockSpec(memory_space=pltpu.SMEM),
            pl.BlockSpec(memory_space=pl.ANY),
        ],
        out_specs=pl.BlockSpec(memory_space=pl.ANY),
        scratch_shapes=[
            pltpu.VMEM(shape, blocks.dtype),
            pltpu.SemaphoreType.DMA((count,)),
            pltpu.SemaphoreType.DMA((count,)),
        ],
        name="gather",
    )(index, blocks)


def on_device(
    source, tiles, tile_slot, tile_dst, send_index, send_count, polar_tiles, polar_src, polar_dst
):
    owners = lax.axis_size("band")
    width = tiles.shape[1]
    feats = source.shape[1]
    per_owner = send_index.shape[1] // owners
    blocks = source.reshape(-1, width, feats)
    outgoing = gather_blocks(send_index, blocks)
    received = lax.all_to_all(
        outgoing.reshape(owners, per_owner, width, feats),
        "band",
        split_axis=0,
        concat_axis=0,
        tiled=True,
    )
    arrived = received.reshape(owners * per_owner, width, feats)
    caps = PB_DEV * owners
    cap_part = block_matmul(
        plan(polar_dst, polar_src, caps), polar_tiles, blocks, caps, jnp.float32, "cap"
    )
    own_cap = lax.psum_scatter(cap_part, "band", scatter_dimension=0, tiled=True)
    polar_cap = own_cap.reshape(PB_DEV * width, feats).astype(jnp.bfloat16)
    rounded = block_matmul(
        plan(tile_dst, tile_slot, TB_DEV), tiles, arrived, TB_DEV, jnp.bfloat16, "field"
    ).reshape(TB_DEV // owners, owners, width, feats)
    placed = lax.all_to_all(rounded, "band", split_axis=1, concat_axis=0, tiled=True)
    model_field = placed.reshape(TB_DEV * width, feats)
    return (model_field, polar_cap)


def solution(mesh):
    placed = (
        P(("grp", "band"), None),
        P("band", None, None),
        P("band"),
        P("band"),
        P("band", None),
        P("band", None),
        P("band", None, None),
        P("band"),
        P("band"),
    )
    return jax.shard_map(
        on_device,
        mesh=mesh,
        in_specs=placed,
        out_specs=(P(("grp", "band"), None), P(("grp", "band"), None)),
        check_vma=False,
    )
```

time: 632 us -> 334 us (0.53)
  other arithmetic: 225 us -> 5.41 us
  local copies, waits for them, and re-layouts: 105 us -> 12.3 us
  matrix products: 77.5 us -> 0 us
  Pallas kernels: 0 us -> 50.1 us
  waiting for transfers between devices: 191 us -> 240 us
    scatter-add x9 -> x0, other arithmetic: 212 us -> none  [the longest x8 170 us: accumulate(): return (total.at[places].add(products), None)]
    dot_general x9 -> x0, matrix products: 77.5 us -> none  [the longest x8 66.5 us: accumulate(): jnp.einsum('tps,tsf->tpf', weights, inputs, preferred_element_type=jnp.fl...]
    gather x10 -> x0, local copies, waits for them, and re-layouts: 66.5 us -> none  [the longest x8 48.2 us: accumulate(): inputs = arrived[slots]]
    pallas_call x0 -> x3, Pallas kernels: none -> 50.1 us  [the longest x2 44.4 us: block_matmul(): pl.pallas_call(block_kernel if rounds else cap_kernel, out_shape=jax.Shap...]
    reduce_scatter x1, waiting for transfers between devices: 76.5 us -> 119 us  [on_device(): lax.psum_scatter(cap_part, 'band', scatter_dimension=0, tiled=True)]
    dot_general x1 -> x0, local copies, waits for them, and re-layouts: 22.8 us -> none  [on_device(): jnp.einsum('tps,tsf->tpf', polar_tiles, polar_inputs, preferred_element_t...]
    all_to_all x1, waiting for transfers between devices: 0.01 us -> 9.59 us  [on_device(): lax.all_to_all(rounded, 'band', split_axis=1, concat_axis=0, tiled=True)]
    broadcast_in_dim x2 -> x0, local copies, waits for them, and re-layouts: 7.91 us -> none  [the longest x1 5.05 us: on_device(): jnp.zeros((TB_DEV, width, feats), jnp.float32)]
  transfers between devices with their start and end apart: 3 -> 3, of which waited for: 2 -> 3; matrix products, arithmetic and copies ran while one was open for 15% -> 2% of each run, Pallas kernels for 0% -> 4%
where the time goes in v1:
time: 334 us
  waiting for transfers between devices  240 us (72%)
  Pallas kernels  50.1 us (15%)
  between operations  14.1 us (4%)
  local copies, waits for them, and re-layouts  12.3 us (4%)
  starting transfers between devices  11.6 us (3%)
  other arithmetic  5.41 us (2%)
    reduce_scatter x1, waiting for transfers between devices, on_device(): lax.psum_scatter(cap_part, 'band', scatter_dimension=0, tiled=True)  119 us
    all_to_all x1, waiting for transfers between devices, on_device(): lax.all_to_all(outgoing.reshape(owners, per_owner, width, feats), 'band',...  112 us
    pallas_call x2, Pallas kernels, block_matmul(): pl.pallas_call(block_kernel if rounds else cap_kernel, out_shape=jax.Shap...  44.4 us
    all_to_all x1, waiting for transfers between devices, on_device(): lax.all_to_all(rounded, 'band', split_axis=1, concat_axis=0, tiled=True)  9.59 us
  transfers between devices with their start and end apart: 3, of which 3 were waited for; matrix products, arithmetic and copies ran while one was open for 2% of the time, Pallas kernels for 4%

profile of v1, /device:TPU:13, one launch (start us, length us, event | category | flops | bytes accessed | tf_op | source)
XLA Modules:
  0.0 333.8 jit_solution(12616135279978431834)
XLA Ops:
  7.2 5.7 %gather.1 = bf16[32,128,640]{2,1,0:T(8,128)(2,1)} custom-call(s32[1,32]{1,0:T(1,128)} %index.1, bf16[64,128,640]{2,1,0:T(8,128)(2,1)} %bitcast.11), custom_call_target="tpu_custom_call" | custom-call | tf_op jit(solution)/shard_map/gather/pallas_call | solution.py:112
  12.9 6.6 %all-to-all-start = ((bf16[16,2,128,640]{3,2,1,0:T(8,128)(2,1)}), bf16[16,2,128,640]{3,2,1,0:T(8,128)(2,1)}, u32[]{:S(2)}, u32[]{:S(2)}) async-start(bf16[16,2,128,640]{3,2,1,0:T(8,128)(2,1)} %bitcast.13), calls=%async_computation | async-start | bytes 10485760 | tf_op jit(solution)/shard_map/all_to_all | solution.py:138
  19.5 0.1 convert_reduce_fusion.2
  19.7 0.1 select_reduce_fusion.5
  19.8 0.7 slice.6.total
  20.4 0.7 convert_reduce_fusion.3.dst_at
  21.1 0.1 select_reduce_fusion.4
  21.2 0.2 convert_reduce_fusion
  21.4 0.8 select_reduce_fusion
  22.2 112.3 %all-to-all-done = bf16[16,2,128,640]{3,2,1,0:T(8,128)(2,1)} async-done(((bf16[16,2,128,640]{3,2,1,0:T(8,128)(2,1)}), bf16[16,2,128,640]{3,2,1,0:T(8,128)(2,1)}, u32[]{:S(2)}, u32[]{:S(2)}) %all-to-all-start) | async-done | bytes 5242912 | tf_op jit(solution)/shard_map/all_to_all | solution.py:138
  134.5 30.1 %field.1 = bf16[32,128,640]{2,1,0:T(8,128)(2,1)} custom-call(s32[384]{0:T(512)} %get-tuple-element.3.tile_at, s32[384]{0:T(512)} %get-tuple-element.2.slot_at, s32[96]{0:T(128)} %convert_reduce_fusion.3.dst_at, s32[1]{0:T(128)} %slice.6.total, bf16[256,128,128]{2,1,0:T(8,128)(2,1)} %tiles.2, bf16[32,128,640]{2,1,0:T(8,128)(2,1)} %bitcast.2.inputs), custom_call_target="tpu_custom_call" | custom-call | flops 10737418240 | bytes 24117248 | tf_op jit(solution)/shard_map/field/pallas_call | solution.py:74
  164.6 5.6 %copy.12 = bf16[2,16,128,640]{3,2,0,1:T(8,128)(2,1)} copy(bf16[2,16,128,640]{3,2,1,0:T(8,128)(2,1)} %bitcast.14) | data formatting | bytes 10485760 | tf_op jit(solution)/shard_map/reshape | solution.py:154
  170.2 4.9 %all-to-all-start.1 = ((bf16[2,16,128,640]{3,2,0,1:T(8,128)(2,1)}), bf16[2,16,128,640]{3,2,0,1:T(8,128)(2,1)}, u32[]{:S(2)}, u32[]{:S(2)}) async-start(bf16[2,16,128,640]{3,2,0,1:T(8,128)(2,1)} %copy.12), calls=%async_computation.1 | async-start | bytes 10485760 | tf_op jit(solution)/shard_map/all_to_all | solution.py:155
  175.2 0.1 convert_reduce_fusion.5
  175.3 0.1 select_reduce_fusion.7
  175.4 0.7 slice.7.total
  176.1 0.6 convert_reduce_fusion.4.dst_at
  176.6 0.2 convert_reduce_fusion.1
  176.9 0.7 select_reduce_fusion.2
  177.6 14.3 %cap.1 = f32[16,128,640]{2,1,0:T(8,128)} custom-call(s32[128]{0:T(128)} %get-tuple-element.5.tile_at, s32[128]{0:T(128)} %get-tuple-element.4.slot_at, s32[32]{0:T(128)} %convert_reduce_fusion.4.dst_at, s32[1]{0:T(128)} %slice.7.total, bf16[64,128,128]{2,1,0:T(8,128)(2,1)} %tiles.3, bf16[64,128,640]{2,1,0:T(8,128)(2,1)} %bitcast.12), custom_call_target="tpu_custom_call" | custom-call | flops 2684354560 | bytes 17825792 | tf_op jit(solution)/shard_map/cap/pallas_call | solution.py:74
  191.9 118.5 %reduce-scatter.2.cloned.1.call-done = f32[1,128,640]{2,1,0:T(8,128)} async-done(((f32[16,128,640]{2,1,0:T(8,128)}), f32[1,128,640]{2,1,0:T(8,128)}) %reduce-scatter.2.cloned.1.call-update) | async-done | bytes 327696 | tf_op jit(solution)/shard_map/reduce_scatter | solution.py:150
  310.4 1.7 convert_bitcast_fusion
  312.1 9.6 %all-to-all-done.1 = bf16[2,16,128,640]{3,2,0,1:T(8,128)(2,1)} async-done(((bf16[2,16,128,640]{3,2,0,1:T(8,128)(2,1)}), bf16[2,16,128,640]{3,2,0,1:T(8,128)(2,1)}, u32[]{:S(2)}, u32[]{:S(2)}) %all-to-all-start.1) | async-done | bytes 5242912 | tf_op jit(solution)/shard_map/all_to_all | solution.py:155
  321.7 5.3 %copy.14 = bf16[4096,640]{1,0:T(8,128)(2,1)} copy(bf16[4096,640]{1,0:T(8,128)(2,1)} %bitcast.6) | data formatting | bytes 10485760
  (17 shorter events, 0.2 us)
Async XLA Ops:
  12.9 6.6 %copy-start = (s32[256]{0:T(256)S(1)}, s32[256]{0:T(256)}, u32[]{:S(2)}) copy-start(s32[256]{0:T(256)} %param.12) | copy-start | bytes 3076
  12.9 8.5 %copy-start.1 = (s32[256]{0:T(256)S(1)}, s32[256]{0:T(256)}, u32[]{:S(2)}) copy-start(s32[256]{0:T(256)} %param.11) | copy-start | bytes 3076
  12.9 121.5 %all-to-all-start = ((bf16[16,2,128,640]{3,2,1,0:T(8,128)(2,1)}), bf16[16,2,128,640]{3,2,1,0:T(8,128)(2,1)}, u32[]{:S(2)}, u32[]{:S(2)}) async-start(bf16[16,2,128,640]{3,2,1,0:T(8,128)(2,1)} %bitcast.13), calls=%async_computation | async-start | bytes 10485760 | tf_op jit(solution)/shard_map/all_to_all | solution.py:138
  170.2 5.0 %copy-start.3 = (s32[64]{0:T(128)S(1)}, s32[64]{0:T(128)}, u32[]{:S(2)}) copy-start(s32[64]{0:T(128)} %param.16) | copy-start | bytes 772
  170.2 6.7 %copy-start.2 = (s32[64]{0:T(128)S(1)}, s32[64]{0:T(128)}, u32[]{:S(2)}) copy-start(s32[64]{0:T(128)} %param.15) | copy-start | bytes 772
  170.2 151.5 %all-to-all-start.1 = ((bf16[2,16,128,640]{3,2,0,1:T(8,128)(2,1)}), bf16[2,16,128,640]{3,2,0,1:T(8,128)(2,1)}, u32[]{:S(2)}, u32[]{:S(2)}) async-start(bf16[2,16,128,640]{3,2,0,1:T(8,128)(2,1)} %copy.12), calls=%async_computation.1 | async-start | bytes 10485760 | tf_op jit(solution)/shard_map/all_to_all | solution.py:155
  175.1 135.3 %reduce-scatter.2.cloned.1.call-start = ((), (), s32[]{:S(2)}) async-start(), calls=%async_computation.3 | async-start | bytes 5570560 | tf_op jit(solution)/shard_map/reduce_scatter | solution.py:150
Sparse Core Ops, SparseCore 0:
  192.0 118.3 reduce-scatter.1

commit v2 on v1

--- a/solution.py
+++ b/solution.py
@@ -67,15 +67,20 @@
     block_kernel(tile_at, slot_at, dst_at, total, tiles, inputs, out, out)
 
 
-def block_matmul(tables, tiles, inputs, blocks, dtype, name):
+def after_kernel(tile_at, slot_at, dst_at, total, tiles, inputs, before, out, acc):
+    block_kernel(tile_at, slot_at, dst_at, total, tiles, inputs, out, acc)
+
+
+def block_matmul(tables, tiles, inputs, blocks, dtype, name, before=()):
     count, width, _ = tiles.shape
     feats = inputs.shape[2]
     rounds = dtype != jnp.float32
     return pl.pallas_call(
-        block_kernel if rounds else cap_kernel,
+        after_kernel if before else block_kernel if rounds else cap_kernel,
         out_shape=jax.ShapeDtypeStruct((blocks, width, feats), dtype),
         in_specs=[pl.BlockSpec(memory_space=pltpu.SMEM)] * 4
-        + [pl.BlockSpec(memory_space=pltpu.VMEM)] * 2,
+        + [pl.BlockSpec(memory_space=pltpu.VMEM)] * 2
+        + [pl.BlockSpec(memory_space=pl.ANY)] * len(before),
         out_specs=pl.BlockSpec(memory_space=pltpu.VMEM),
         scratch_shapes=[pltpu.VMEM((blocks, width, feats), jnp.float32)] if rounds else [],
         compiler_params=pltpu.CompilerParams(vmem_limit_bytes=56 * 1024 * 1024),
@@ -85,45 +90,61 @@
             transcendentals=0,
         ),
         name=name,
-    )(*tables, tiles, inputs)
-
-
-def gather_kernel(index, blocks, out, held, in_sem, out_sem):
-    count = out.shape[0]
+    )(*tables, tiles, inputs, *before)
+
+
+def gather_kernel(cuts, index, blocks, *refs):
+    parts = len(cuts)
+    outs = refs[:parts]
+    held, in_sem, out_sem = refs[parts:]
+    count = held.shape[0]
     reads = [
         pltpu.make_async_copy(blocks.at[index[0, i]], held.at[i], in_sem.at[i])
         for i in range(count)
     ]
-    writes = [
-        pltpu.make_async_copy(held.at[i], out.at[i], out_sem.at[i]) for i in range(count)
-    ]
     for copy in reads:
         copy.start()
-    for read, write in zip(reads, writes):
-        read.wait()
-        write.start()
+    for copy in reads:
+        copy.wait()
+    writes = []
+    for c, (low, high) in enumerate(cuts):
+        for i in range(count):
+            writes.append(
+                pltpu.make_async_copy(
+                    held.at[i, :, low:high], outs[c].at[i], out_sem.at[c * count + i]
+                )
+            )
+            writes[-1].start()
     for copy in writes:
         copy.wait()
 
 
-def gather_blocks(index, blocks):
+def gather_blocks(index, blocks, cuts):
     count = index.shape[1]
-    shape = (count,) + blocks.shape[1:]
+    width = blocks.shape[1]
     return pl.pallas_call(
-        gather_kernel,
-        out_shape=jax.ShapeDtypeStruct(shape, blocks.dtype),
+        functools.partial(gather_kernel, cuts),
+        out_shape=[
+            jax.ShapeDtypeStruct((count, width, high - low), blocks.dtype) for low, high in cuts
+        ],
         in_specs=[
             pl.BlockSpec(memory_space=pltpu.SMEM),
             pl.BlockSpec(memory_space=pl.ANY),
         ],
-        out_specs=pl.BlockSpec(memory_space=pl.ANY),
+        out_specs=[pl.BlockSpec(memory_space=pl.ANY)] * len(cuts),
         scratch_shapes=[
-            pltpu.VMEM(shape, blocks.dtype),
+            pltpu.VMEM((count,) + blocks.shape[1:], blocks.dtype),
             pltpu.SemaphoreType.DMA((count,)),
-            pltpu.SemaphoreType.DMA((count,)),
+            pltpu.SemaphoreType.DMA((count * len(cuts),)),
         ],
         name="gather",
     )(index, blocks)
+
+
+def feature_cuts(feats):
+    lanes = 128
+    half = -(-feats // (2 * lanes)) * lanes
+    return ((0, half), (half, feats)) if half < feats else ((0, feats),)
 
 
 def on_device(
@@ -134,27 +155,41 @@
     feats = source.shape[1]
     per_owner = send_index.shape[1] // owners
     blocks = source.reshape(-1, width, feats)
-    outgoing = gather_blocks(send_index, blocks)
-    received = lax.all_to_all(
-        outgoing.reshape(owners, per_owner, width, feats),
-        "band",
-        split_axis=0,
-        concat_axis=0,
-        tiled=True,
-    )
-    arrived = received.reshape(owners * per_owner, width, feats)
+    cuts = feature_cuts(feats)
+    received = []
+    for low_high, outgoing in zip(cuts, gather_blocks(send_index, blocks, cuts)):
+        span = low_high[1] - low_high[0]
+        got = lax.all_to_all(
+            outgoing.reshape(owners, per_owner, width, span),
+            "band",
+            split_axis=0,
+            concat_axis=0,
+            tiled=True,
+        )
+        received.append(got.reshape(owners * per_owner, width, span))
     caps = PB_DEV * owners
     cap_part = block_matmul(
         plan(polar_dst, polar_src, caps), polar_tiles, blocks, caps, jnp.float32, "cap"
     )
     own_cap = lax.psum_scatter(cap_part, "band", scatter_dimension=0, tiled=True)
     polar_cap = own_cap.reshape(PB_DEV * width, feats).astype(jnp.bfloat16)
-    rounded = block_matmul(
-        plan(tile_dst, tile_slot, TB_DEV), tiles, arrived, TB_DEV, jnp.bfloat16, "field"
-    ).reshape(TB_DEV // owners, owners, width, feats)
-    placed = lax.all_to_all(rounded, "band", split_axis=1, concat_axis=0, tiled=True)
-    model_field = placed.reshape(TB_DEV * width, feats)
-    return (model_field, polar_cap)
+    turn = TB_DEV // owners
+    target = (tile_dst % owners) * turn + tile_dst // owners
+    tables = plan(target, tile_slot, TB_DEV)
+    placed = []
+    for arrived in received:
+        span = arrived.shape[2]
+        before = (cap_part,)
+        rounded = block_matmul(tables, tiles, arrived, TB_DEV, jnp.bfloat16, "field", before)
+        sent = lax.all_to_all(
+            rounded.reshape(owners, turn, width, span),
+            "band",
+            split_axis=0,
+            concat_axis=0,
+            tiled=True,
+        )
+        placed.append(sent.reshape(TB_DEV * width, span))
+    return (jnp.concatenate(placed, axis=1), polar_cap)
 
 
 def solution(mesh):

time: 334 us -> 316 us (0.946)
  waiting for transfers between devices: 240 us -> 153 us
  blocking collectives: 0 us -> 53.9 us
  Pallas kernels: 50.1 us -> 65.3 us
  local copies, waits for them, and re-layouts: 12.3 us -> 4.36 us
  other arithmetic: 5.41 us -> 10 us
    reduce_scatter x1, waiting for transfers between devices: 119 us -> 34.7 us  [on_device(): lax.psum_scatter(cap_part, 'band', scatter_dimension=0, tiled=True)]
    all_to_all x0 -> x1, blocking collectives: none -> 53.9 us  [on_device(): lax.all_to_all(outgoing.reshape(owners, per_owner, width, span), 'band',...]
    pallas_call x3 -> x4, Pallas kernels: 50.1 us -> 65.3 us  [the longest x3 58.9 us: block_matmul(): pl.pallas_call(after_kernel if before else block_kernel if rounds else ca...]
    reshape x1 -> x0, local copies, waits for them, and re-layouts: 5.62 us -> none  [on_device(): rounded = block_matmul(plan(tile_dst, tile_slot, TB_DEV), tiles, arrived,...]
    concatenate x0 -> x1, other arithmetic: none -> 4.49 us  [on_device(): return (jnp.concatenate(placed, axis=1), polar_cap)]
    all_to_all x2 -> x3, waiting for transfers between devices: 122 us -> 118 us  [the longest x2 87.7 us: on_device(): lax.all_to_all(rounded.reshape(owners, turn, width, span), 'band', split_...]
    all_to_all x2 -> x3, starting transfers between devices: 11.5 us -> 14.9 us  [the longest x2 9.68 us: on_device(): lax.all_to_all(rounded.reshape(owners, turn, width, span), 'band', split_...]
  transfers between devices with their start and end apart: 3 -> 4, of which waited for: 3 -> 4; matrix products, arithmetic and copies ran while one was open for 2% -> 2% of each run, Pallas kernels for 4% -> 19%
where the time goes in v2:
time: 316 us
  waiting for transfers between devices  153 us (48%)
  Pallas kernels  65.3 us (21%)
  blocking collectives  53.9 us (17%)
  starting transfers between devices  14.9 us (5%)
  between operations  14.1 us (4%)
  other arithmetic  10 us (3%)
  local copies, waits for them, and re-layouts  4.36 us (1%)
    all_to_all x2, waiting for transfers between devices, on_device(): lax.all_to_all(rounded.reshape(owners, turn, width, span), 'band', split_...  87.7 us
    pallas_call x3, Pallas kernels, block_matmul(): pl.pallas_call(after_kernel if before else block_kernel if rounds else ca...  58.9 us
    all_to_all x1, blocking collectives, on_device(): lax.all_to_all(outgoing.reshape(owners, per_owner, width, span), 'band',...  53.9 us
    reduce_scatter x1, waiting for transfers between devices, on_device(): lax.psum_scatter(cap_part, 'band', scatter_dimension=0, tiled=True)  34.7 us
    all_to_all x1, waiting for transfers between devices, on_device(): lax.all_to_all(outgoing.reshape(owners, per_owner, width, span), 'band',...  29.9 us
    all_to_all x2, starting transfers between devices, on_device(): lax.all_to_all(rounded.reshape(owners, turn, width, span), 'band', split_...  9.68 us
    pallas_call x1, Pallas kernels, gather_blocks(): pl.pallas_call(functools.partial(gather_kernel, cuts), out_shape=[jax.Sha...  6.38 us
  transfers between devices with their start and end apart: 4, of which 4 were waited for; matrix products, arithmetic and copies ran while one was open for 2% of the time, Pallas kernels for 19%

profile of v2, /device:TPU:13, one launch (start us, length us, event | category | flops | bytes accessed | tf_op | source)
XLA Modules:
  0.0 315.5 jit_solution(15447550394507712432)
XLA Ops:
  7.2 6.4 %gather.1 = (bf16[32,128,384]{2,1,0:T(8,128)(2,1)}, bf16[32,128,256]{2,1,0:T(8,128)(2,1)}) custom-call(s32[1,32]{1,0:T(1,128)} %index.1, bf16[64,128,640]{2,1,0:T(8,128)(2,1)} %bitcast.11), custom_call_target="tpu_custom_call" | custom-call | tf_op jit(solution)/shard_map/gather/pallas_call | solution.py:125
  13.6 53.9 %all_to_all.20 = bf16[16,2,128,256]{3,2,1,0:T(8,128)(2,1)} all-to-all(bf16[16,2,128,256]{3,2,1,0:T(8,128)(2,1)} %bitcast.20), channel_id=1, replica_groups=mesh['grp'=2,'band'=16] {'band'}, dimensions={0} | all-to-all | bytes 4194304 | tf_op jit(solution)/shard_map/all_to_all | solution.py:162
  67.5 5.2 %all-to-all-start = ((bf16[16,2,128,384]{3,2,1,0:T(8,128)(2,1)}), bf16[16,2,128,384]{3,2,1,0:T(8,128)(2,1)S(1)}, u32[]{:S(2)}, u32[]{:S(2)}) async-start(bf16[16,2,128,384]{3,2,1,0:T(8,128)(2,1)} %bitcast.18), calls=%async_computation | async-start | bytes 6291456 | tf_op jit(solution)/shard_map/all_to_all | solution.py:162
  72.9 0.6 slice.7.total
  73.8 0.7 slice.6.total
  74.4 0.7 convert_reduce_fusion.4.dst_at
  75.1 0.7 convert_reduce_fusion.3.dst_at
  76.1 0.7 select_reduce_fusion.2
  76.8 0.2 convert_reduce_fusion
  77.0 0.8 select_reduce_fusion
  77.8 14.0 %cap.1.before = f32[16,128,640]{2,1,0:T(8,128)} custom-call(s32[128]{0:T(128)} %get-tuple-element.9.tile_at, s32[128]{0:T(128)} %get-tuple-element.8.slot_at, s32[32]{0:T(128)} %convert_reduce_fusion.4.dst_at, s32[1]{0:T(128)} %slice.7.total, bf16[64,128,128]{2,1,0:T(8,128)(2,1)} %tiles.3, bf16[64,128,640]{2,1,0:T(8,128)(2,1)} %bitcast.12), custom_call_target="tpu_custom_call" | custom-call | flops 2684354560 | bytes 17825792 | tf_op jit(solution)/shard_map/cap/pallas_call | solution.py:78
  91.8 20.9 %field.3 = bf16[32,128,256]{2,1,0:T(8,128)(2,1)} custom-call(s32[384]{0:T(512)} %get-tuple-element.7.tile_at, s32[384]{0:T(512)} %get-tuple-element.6.slot_at, s32[96]{0:T(128)} %convert_reduce_fusion.3.dst_at, s32[1]{0:T(128)} %slice.6.total, bf16[256,128,128]{2,1,0:T(8,128)(2,1)} %tiles.5, bf16[32,128,256]{2,1,0:T(8,128)(2,1)} %bitcast.14, ...), custom_call_target="tpu_custom_call" | custom-call | flops 4294967296 | bytes 14680064 | tf_op jit(solution)/shard_map/field/pallas_call | solution.py:78
  112.7 29.9 %all-to-all-done = bf16[16,2,128,384]{3,2,1,0:T(8,128)(2,1)S(1)} async-done(((bf16[16,2,128,384]{3,2,1,0:T(8,128)(2,1)}), bf16[16,2,128,384]{3,2,1,0:T(8,128)(2,1)S(1)}, u32[]{:S(2)}, u32[]{:S(2)}) %all-to-all-start) | async-done | bytes 3145760 | tf_op jit(solution)/shard_map/all_to_all | solution.py:162
  142.5 1.7 copy-done.1
  144.2 4.8 %all-to-all-start.3 = ((bf16[16,2,128,256]{3,2,1,0:T(8,128)(2,1)}), bf16[16,2,128,256]{3,2,1,0:T(8,128)(2,1)S(1)}, u32[]{:S(2)}, u32[]{:S(2)}) async-start(bf16[16,2,128,256]{3,2,1,0:T(8,128)(2,1)} %bitcast.16), calls=%async_computation.3 | async-start | bytes 4194304 | tf_op jit(solution)/shard_map/all_to_all | solution.py:184
  149.1 0.7 reduce-scatter.2.cloned.1.call-update
  149.7 24.1 %field.2 = bf16[32,128,384]{2,1,0:T(8,128)(2,1)} custom-call(s32[384]{0:T(512)} %get-tuple-element.7.tile_at, s32[384]{0:T(512)} %get-tuple-element.6.slot_at, s32[96]{0:T(128)} %convert_reduce_fusion.3.dst_at, s32[1]{0:T(128)} %slice.6.total, bf16[256,128,128]{2,1,0:T(8,128)(2,1)} %tiles.5, bf16[32,128,384]{2,1,0:T(8,128)(2,1)} %bitcast.17, ...), custom_call_target="tpu_custom_call" | custom-call | flops 6442450944 | bytes 17825792 | tf_op jit(solution)/shard_map/field/pallas_call | solution.py:78
  173.8 43.6 %all-to-all-done.3 = bf16[16,2,128,256]{3,2,1,0:T(8,128)(2,1)S(1)} async-done(((bf16[16,2,128,256]{3,2,1,0:T(8,128)(2,1)}), bf16[16,2,128,256]{3,2,1,0:T(8,128)(2,1)S(1)}, u32[]{:S(2)}, u32[]{:S(2)}) %all-to-all-start.3) | async-done | bytes 2097184 | tf_op jit(solution)/shard_map/all_to_all | solution.py:184
  217.4 1.4 copy-done
  218.7 4.9 %all-to-all-start.1 = ((bf16[16,2,128,384]{3,2,1,0:T(8,128)(2,1)}), bf16[16,2,128,384]{3,2,1,0:T(8,128)(2,1)S(1)}, u32[]{:S(2)}, u32[]{:S(2)}) async-start(bf16[16,2,128,384]{3,2,1,0:T(8,128)(2,1)} %bitcast.19), calls=%async_computation.1 | async-start | bytes 6291456 | tf_op jit(solution)/shard_map/all_to_all | solution.py:184
  223.6 34.7 %reduce-scatter.2.cloned.1.call-done = f32[1,128,640]{2,1,0:T(8,128)} async-done(((f32[16,128,640]{2,1,0:T(8,128)}), f32[1,128,640]{2,1,0:T(8,128)}) %reduce-scatter.2.cloned.1.call-update) | async-done | bytes 327696 | tf_op jit(solution)/shard_map/reduce_scatter | solution.py:174
  258.4 1.7 convert_bitcast_fusion
  260.1 44.1 %all-to-all-done.1 = bf16[16,2,128,384]{3,2,1,0:T(8,128)(2,1)S(1)} async-done(((bf16[16,2,128,384]{3,2,1,0:T(8,128)(2,1)}), bf16[16,2,128,384]{3,2,1,0:T(8,128)(2,1)S(1)}, u32[]{:S(2)}, u32[]{:S(2)}) %all-to-all-start.1) | async-done | bytes 3145760 | tf_op jit(solution)/shard_map/all_to_all | solution.py:184
  304.2 4.5 %pad_maximum_fusion = bf16[4096,640]{1,0:T(8,128)(2,1)} fusion(bf16[4096,256]{1,0:T(8,128)(2,1)} %bitcast.15, bf16[4096,384]{1,0:T(8,128)(2,1)S(1)} %bitcast.13), kind=kLoop, calls=%fused_computation | loop fusion | flops 10485760 | bytes 10485760 | tf_op jit(solution)/shard_map/concatenate | solution.py:192
  (25 shorter events, 0.9 us)
Async XLA Ops:
  67.5 5.2 %copy-start.5 = (s32[64]{0:T(128)S(1)}, s32[64]{0:T(128)}, u32[]{:S(2)}) copy-start(s32[64]{0:T(128)} %param.16) | copy-start | bytes 772
  67.5 6.0 %copy-start.3 = (s32[256]{0:T(256)S(1)}, s32[256]{0:T(256)}, u32[]{:S(2)}) copy-start(s32[256]{0:T(256)} %param.12) | copy-start | bytes 3076
  67.5 8.7 %copy-start.4 = (s32[64]{0:T(128)S(1)}, s32[64]{0:T(128)}, u32[]{:S(2)}) copy-start(s32[64]{0:T(128)} %param.15) | copy-start | bytes 772
  67.5 9.6 %copy-start.2 = (s32[256]{0:T(256)S(1)}, s32[256]{0:T(256)}, u32[]{:S(2)}) copy-start(s32[256]{0:T(256)} %param.11) | copy-start | bytes 3076
  67.5 75.1 %all-to-all-start = ((bf16[16,2,128,384]{3,2,1,0:T(8,128)(2,1)}), bf16[16,2,128,384]{3,2,1,0:T(8,128)(2,1)S(1)}, u32[]{:S(2)}, u32[]{:S(2)}) async-start(bf16[16,2,128,384]{3,2,1,0:T(8,128)(2,1)} %bitcast.18), calls=%async_computation | async-start | bytes 6291456 | tf_op jit(solution)/shard_map/all_to_all | solution.py:162
  142.5 1.7 copy-start.1
  144.2 73.1 %all-to-all-start.3 = ((bf16[16,2,128,256]{3,2,1,0:T(8,128)(2,1)}), bf16[16,2,128,256]{3,2,1,0:T(8,128)(2,1)S(1)}, u32[]{:S(2)}, u32[]{:S(2)}) async-start(bf16[16,2,128,256]{3,2,1,0:T(8,128)(2,1)} %bitcast.16), calls=%async_computation.3 | async-start | bytes 4194304 | tf_op jit(solution)/shard_map/all_to_all | solution.py:184
  149.0 109.4 %reduce-scatter.2.cloned.1.call-start = ((), (), s32[]{:S(2)}) async-start(), calls=%async_computation.5 | async-start | bytes 5570560 | tf_op jit(solution)/shard_map/reduce_scatter | solution.py:174
  217.4 1.4 copy-start
  218.7 85.4 %all-to-all-start.1 = ((bf16[16,2,128,384]{3,2,1,0:T(8,128)(2,1)}), bf16[16,2,128,384]{3,2,1,0:T(8,128)(2,1)S(1)}, u32[]{:S(2)}, u32[]{:S(2)}) async-start(bf16[16,2,128,384]{3,2,1,0:T(8,128)(2,1)} %bitcast.19), calls=%async_computation.1 | async-start | bytes 6291456 | tf_op jit(solution)/shard_map/all_to_all | solution.py:184
Sparse Core Ops, SparseCore 0:
  154.2 104.0 reduce-scatter.1

commit v3 on v2

--- a/solution.py
+++ b/solution.py
@@ -63,7 +63,7 @@
         out[...] = acc[...].astype(out.dtype)
 
 
-def cap_kernel(tile_at, slot_at, dst_at, total, tiles, inputs, out):
+def cap_kernel(tile_at, slot_at, dst_at, total, tiles, inputs, before, out):
     block_kernel(tile_at, slot_at, dst_at, total, tiles, inputs, out, out)
 
 
@@ -76,7 +76,7 @@
     feats = inputs.shape[2]
     rounds = dtype != jnp.float32
     return pl.pallas_call(
-        after_kernel if before else block_kernel if rounds else cap_kernel,
+        after_kernel if rounds else cap_kernel,
         out_shape=jax.ShapeDtypeStruct((blocks, width, feats), dtype),
         in_specs=[pl.BlockSpec(memory_space=pltpu.SMEM)] * 4
         + [pl.BlockSpec(memory_space=pltpu.VMEM)] * 2
@@ -147,6 +147,29 @@
     return ((0, half), (half, feats)) if half < feats else ((0, feats),)
 
 
+def halve(parts, stride):
+    owners = lax.axis_size("band")
+    bit = lax.rem(lax.axis_index("band") // stride, 2)
+    pairs = parts.reshape((-1, 2) + parts.shape[1:])
+    keep = lax.dynamic_index_in_dim(pairs, bit, 1, keepdims=False)
+    send = lax.dynamic_index_in_dim(pairs, 1 - bit, 1, keepdims=False)
+    got = lax.ppermute(send, "band", [(i, i ^ stride) for i in range(owners)])
+    return keep + got
+
+
+def reduce_caps(parts):
+    owners = lax.axis_size("band")
+    stride = 1
+    while stride < 4 and owners % (2 * stride) == 0:
+        parts = halve(parts, stride)
+        stride *= 2
+    groups = [list(range(i, owners, stride)) for i in range(stride)]
+    got = lax.all_to_all(
+        parts, "band", split_axis=0, concat_axis=0, axis_index_groups=groups, tiled=True
+    )
+    return jnp.sum(got, axis=0)
+
+
 def on_device(
     source, tiles, tile_slot, tile_dst, send_index, send_count, polar_tiles, polar_src, polar_dst
 ):
@@ -157,7 +180,8 @@
     blocks = source.reshape(-1, width, feats)
     cuts = feature_cuts(feats)
     received = []
-    for low_high, outgoing in zip(cuts, gather_blocks(send_index, blocks, cuts)):
+    gathered = gather_blocks(send_index, blocks, cuts)
+    for low_high, outgoing in zip(cuts, gathered):
         span = low_high[1] - low_high[0]
         got = lax.all_to_all(
             outgoing.reshape(owners, per_owner, width, span),
@@ -169,9 +193,9 @@
         received.append(got.reshape(owners * per_owner, width, span))
     caps = PB_DEV * owners
     cap_part = block_matmul(
-        plan(polar_dst, polar_src, caps), polar_tiles, blocks, caps, jnp.float32, "cap"
-    )
-    own_cap = lax.psum_scatter(cap_part, "band", scatter_dimension=0, tiled=True)
+        plan(polar_dst, polar_src, caps), polar_tiles, blocks, caps, jnp.float32, "cap", gathered[:1]
+    )
+    own_cap = reduce_caps(cap_part.reshape(owners, PB_DEV * width, feats))
     polar_cap = own_cap.reshape(PB_DEV * width, feats).astype(jnp.bfloat16)
     turn = TB_DEV // owners
     target = (tile_dst % owners) * turn + tile_dst // owners

time: 316 us -> 313 us (level)
  blocking collectives: 53.9 us -> 0 us
  waiting for transfers between devices: 153 us -> 194 us
  starting transfers between devices: 14.9 us -> 28.4 us
  between operations: 14.1 us -> 0.75 us
  other arithmetic: 10 us -> 15.7 us
  local copies, waits for them, and re-layouts: 4.36 us -> 8.18 us
    all_to_all x1 -> x0, blocking collectives: 53.9 us -> none  [on_device(): lax.all_to_all(outgoing.reshape(owners, per_owner, width, span), 'band',...]
    ppermute x0 -> x2, waiting for transfers between devices: none -> 51.8 us  [halve(): got = lax.ppermute(send, 'band', [(i, i ^ stride) for i in range(owners)])]
    reduce_scatter x1 -> x0, waiting for transfers between devices: 34.7 us -> none  [on_device(): lax.psum_scatter(cap_part, 'band', scatter_dimension=0, tiled=True)]
    all_to_all x1 -> x2, waiting for transfers between devices: 29.9 us -> 46.4 us  [on_device(): lax.all_to_all(outgoing.reshape(owners, per_owner, width, span), 'band',...]
    all_to_all x1 -> x2, starting transfers between devices: 5.17 us -> 11.3 us  [on_device(): lax.all_to_all(outgoing.reshape(owners, per_owner, width, span), 'band',...]
    add x0 -> x2, other arithmetic: none -> 5.4 us  [halve(): return keep + got]
    all_to_all x0 -> x1, waiting for transfers between devices: none -> 4.21 us  [reduce_caps(): lax.all_to_all(parts, 'band', split_axis=0, concat_axis=0, axis_index_gro...]
    all_to_all x0 -> x1, starting transfers between devices: none -> 3.53 us  [reduce_caps(): lax.all_to_all(parts, 'band', split_axis=0, concat_axis=0, axis_index_gro...]
  transfers between devices with their start and end apart: 4 -> 7, of which waited for: 4 -> 6; matrix products, arithmetic and copies ran while one was open for 2% -> 5% of each run, Pallas kernels for 19% -> 19%
where the time goes in v3:
time: 313 us; the launch traced here: 312 us
  waiting for transfers between devices  194 us (62%)
  Pallas kernels  65.3 us (21%)
  starting transfers between devices  28.4 us (9%)
  other arithmetic  15.7 us (5%)
  local copies, waits for them, and re-layouts  8.18 us (3%)
    all_to_all x2, waiting for transfers between devices, on_device(): lax.all_to_all(rounded.reshape(owners, turn, width, span), 'band', split_...  91.1 us
    pallas_call x3, Pallas kernels, block_matmul(): pl.pallas_call(after_kernel if rounds else cap_kernel, out_shape=jax.Shap...  58.9 us
    ppermute x2, waiting for transfers between devices, halve(): got = lax.ppermute(send, 'band', [(i, i ^ stride) for i in range(owners)])  51.8 us
    all_to_all x2, waiting for transfers between devices, on_device(): lax.all_to_all(outgoing.reshape(owners, per_owner, width, span), 'band',...  46.4 us
    all_to_all x2, starting transfers between devices, on_device(): lax.all_to_all(rounded.reshape(owners, turn, width, span), 'band', split_...  12.9 us
    all_to_all x2, starting transfers between devices, on_device(): lax.all_to_all(outgoing.reshape(owners, per_owner, width, span), 'band',...  11.3 us
    pallas_call x1, Pallas kernels, gather_blocks(): pl.pallas_call(functools.partial(gather_kernel, cuts), out_shape=[jax.Sha...  6.38 us
  transfers between devices with their start and end apart: 7, of which 6 were waited for; matrix products, arithmetic and copies ran while one was open for 5% of the time, Pallas kernels for 19%

profile of v3, /device:TPU:13, one launch (start us, length us, event | category | flops | bytes accessed | tf_op | source)
XLA Modules:
  0.0 311.8 jit_solution(14789466089860327631)
XLA Ops:
  0.6 6.4 %gather.1 = (bf16[32,128,384]{2,1,0:T(8,128)(2,1)}, bf16[32,128,256]{2,1,0:T(8,128)(2,1)}) custom-call(s32[1,32]{1,0:T(1,128)} %index.1, bf16[64,128,640]{2,1,0:T(8,128)(2,1)} %bitcast.21), custom_call_target="tpu_custom_call" | custom-call | tf_op jit(solution)/shard_map/gather/pallas_call | solution.py:125
  7.0 6.5 %all-to-all-start.2 = ((bf16[16,2,128,256]{3,2,1,0:T(8,128)(2,1)}), bf16[16,2,128,256]{3,2,1,0:T(8,128)(2,1)S(1)}, u32[]{:S(2)}, u32[]{:S(2)}) async-start(bf16[16,2,128,256]{3,2,1,0:T(8,128)(2,1)} %bitcast.30), calls=%async_computation.2 | async-start | bytes 4194304 | tf_op jit(solution)/shard_map/all_to_all | solution.py:186
  14.6 46.4 %all-to-all-done.2 = bf16[16,2,128,256]{3,2,1,0:T(8,128)(2,1)S(1)} async-done(((bf16[16,2,128,256]{3,2,1,0:T(8,128)(2,1)}), bf16[16,2,128,256]{3,2,1,0:T(8,128)(2,1)S(1)}, u32[]{:S(2)}, u32[]{:S(2)}) %all-to-all-start.2) | async-done | bytes 2097184 | tf_op jit(solution)/shard_map/all_to_all | solution.py:186
  61.0 1.4 copy-done
  62.4 4.8 %all-to-all-start = ((bf16[16,2,128,384]{3,2,1,0:T(8,128)(2,1)}), bf16[16,2,128,384]{3,2,1,0:T(8,128)(2,1)}, u32[]{:S(2)}, u32[]{:S(2)}) async-start(bf16[16,2,128,384]{3,2,1,0:T(8,128)(2,1)} %bitcast.1), calls=%async_computation | async-start | bytes 6291456 | tf_op jit(solution)/shard_map/all_to_all | solution.py:186
  68.5 13.9 %cap.1.before = f32[16,128,640]{2,1,0:T(8,128)} custom-call(s32[128]{0:T(128)} %get-tuple-element.9.tile_at, s32[128]{0:T(128)} %get-tuple-element.8.slot_at, s32[32]{0:T(128)} %convert_reduce_fusion.4.dst_at, s32[1]{0:T(128)} %slice.7.total, bf16[64,128,128]{2,1,0:T(8,128)(2,1)} %tiles.3, bf16[64,128,640]{2,1,0:T(8,128)(2,1)} %bitcast.22, ...), custom_call_target="tpu_custom_call" | custom-call | flops 2684354560 | bytes 17825792 | tf_op jit(solution)/shard_map/cap/pallas_call | solution.py:78
  82.4 1.9 dynamic-slice_bitcast_fusion
  84.4 5.0 %collective-permute-done = f32[8,128,640]{2,1,0:T(8,128)} collective-permute-done((f32[8,128,640]{2,1,0:T(8,128)S(1)}, f32[8,128,640]{2,1,0:T(8,128)}, u32[]{:S(2)}, u32[]{:S(2)}) %collective-permute-start) | collective-permute-done | bytes 2621472 | tf_op jit(solution)/shard_map/ppermute | solution.py:156
  89.4 2.8 bitcast_add_fusion
  92.2 1.3 dynamic-slice_bitcast_fusion.1
  94.0 46.8 %collective-permute-done.1 = f32[4,128,640]{2,1,0:T(8,128)} collective-permute-done((f32[4,128,640]{2,1,0:T(8,128)}, f32[4,128,640]{2,1,0:T(8,128)}, u32[]{:S(2)}, u32[]{:S(2)}) %collective-permute-start.1) | collective-permute-done | bytes 1310752 | tf_op jit(solution)/shard_map/ppermute | solution.py:156
  140.8 2.6 bitcast_add_fusion.1
  143.4 3.5 %all-to-all-start.4 = ((f32[4,128,640]{2,1,0:T(8,128)}), f32[4,128,640]{2,1,0:T(8,128)S(1)}, u32[]{:S(2)}, u32[]{:S(2)}) async-start(f32[4,128,640]{2,1,0:T(8,128)} %bitcast_add_fusion.1), calls=%async_computation.4 | async-start | bytes 2621440 | tf_op jit(solution)/shard_map/all_to_all | solution.py:167
  149.6 20.9 %field.3 = bf16[32,128,256]{2,1,0:T(8,128)(2,1)} custom-call(s32[384]{0:T(512)} %get-tuple-element.7.tile_at, s32[384]{0:T(512)} %get-tuple-element.6.slot_at, s32[96]{0:T(128)} %convert_reduce_fusion.3.dst_at, s32[1]{0:T(128)} %slice.6.total, bf16[256,128,128]{2,1,0:T(8,128)(2,1)} %tiles.5, bf16[32,128,256]{2,1,0:T(8,128)(2,1)} %bitcast.26, ...), custom_call_target="tpu_custom_call" | custom-call | flops 4294967296 | bytes 14680064 | tf_op jit(solution)/shard_map/field/pallas_call | solution.py:78
  170.5 4.2 %all-to-all-done.4 = f32[4,128,640]{2,1,0:T(8,128)S(1)} async-done(((f32[4,128,640]{2,1,0:T(8,128)}), f32[4,128,640]{2,1,0:T(8,128)S(1)}, u32[]{:S(2)}, u32[]{:S(2)}) %all-to-all-start.4) | async-done | bytes 1310752 | tf_op jit(solution)/shard_map/all_to_all | solution.py:167
  174.7 1.1 copy-done.2
  175.8 8.1 %all-to-all-start.3 = ((bf16[16,2,128,256]{3,2,1,0:T(8,128)(2,1)}), bf16[16,2,128,256]{3,2,1,0:T(8,128)(2,1)S(1)}, u32[]{:S(2)}, u32[]{:S(2)}) async-start(bf16[16,2,128,256]{3,2,1,0:T(8,128)(2,1)} %bitcast.28), calls=%async_computation.3 | async-start | bytes 4194304 | tf_op jit(solution)/shard_map/all_to_all | solution.py:208
  183.9 24.1 %field.2 = bf16[32,128,384]{2,1,0:T(8,128)(2,1)} custom-call(s32[384]{0:T(512)} %get-tuple-element.7.tile_at, s32[384]{0:T(512)} %get-tuple-element.6.slot_at, s32[96]{0:T(128)} %convert_reduce_fusion.3.dst_at, s32[1]{0:T(128)} %slice.6.total, bf16[256,128,128]{2,1,0:T(8,128)(2,1)} %tiles.5, bf16[32,128,384]{2,1,0:T(8,128)(2,1)} %bitcast.2.inputs, ...), custom_call_target="tpu_custom_call" | custom-call | flops 6442450944 | bytes 17825792 | tf_op jit(solution)/shard_map/field/pallas_call | solution.py:78
  208.0 23.3 %all-to-all-done.3 = bf16[16,2,128,256]{3,2,1,0:T(8,128)(2,1)S(1)} async-done(((bf16[16,2,128,256]{3,2,1,0:T(8,128)(2,1)}), bf16[16,2,128,256]{3,2,1,0:T(8,128)(2,1)S(1)}, u32[]{:S(2)}, u32[]{:S(2)}) %all-to-all-start.3) | async-done | bytes 2097184 | tf_op jit(solution)/shard_map/all_to_all | solution.py:208
  231.3 1.3 copy-done.1
  232.6 4.8 %all-to-all-start.1 = ((bf16[16,2,128,384]{3,2,1,0:T(8,128)(2,1)}), bf16[16,2,128,384]{3,2,1,0:T(8,128)(2,1)S(1)}, u32[]{:S(2)}, u32[]{:S(2)}) async-start(bf16[16,2,128,384]{3,2,1,0:T(8,128)(2,1)} %bitcast.29), calls=%async_computation.1 | async-start | bytes 6291456 | tf_op jit(solution)/shard_map/all_to_all | solution.py:208
  237.4 2.1 reduce_sum.149
  239.5 67.8 %all-to-all-done.1 = bf16[16,2,128,384]{3,2,1,0:T(8,128)(2,1)S(1)} async-done(((bf16[16,2,128,384]{3,2,1,0:T(8,128)(2,1)}), bf16[16,2,128,384]{3,2,1,0:T(8,128)(2,1)S(1)}, u32[]{:S(2)}, u32[]{:S(2)}) %all-to-all-start.1) | async-done | bytes 3145760 | tf_op jit(solution)/shard_map/all_to_all | solution.py:208
  307.3 4.5 %pad_maximum_fusion = bf16[4096,640]{1,0:T(8,128)(2,1)} fusion(bf16[4096,256]{1,0:T(8,128)(2,1)} %bitcast.27, bf16[4096,384]{1,0:T(8,128)(2,1)S(1)} %bitcast.23), kind=kLoop, calls=%fused_computation | loop fusion | flops 10485760 | bytes 10485760 | tf_op jit(solution)/shard_map/concatenate | solution.py:216
  (35 shorter events, 5.6 us)
Async XLA Ops:
  7.0 6.5 %copy-start.6 = (s32[64]{0:T(128)S(1)}, s32[64]{0:T(128)}, u32[]{:S(2)}) copy-start(s32[64]{0:T(128)} %param.16) | copy-start | bytes 772
  7.0 54.0 %all-to-all-start.2 = ((bf16[16,2,128,256]{3,2,1,0:T(8,128)(2,1)}), bf16[16,2,128,256]{3,2,1,0:T(8,128)(2,1)S(1)}, u32[]{:S(2)}, u32[]{:S(2)}) async-start(bf16[16,2,128,256]{3,2,1,0:T(8,128)(2,1)} %bitcast.30), calls=%async_computation.2 | async-start | bytes 4194304 | tf_op jit(solution)/shard_map/all_to_all | solution.py:186
  61.0 1.4 copy-start
  61.0 6.9 %copy-start.5 = (s32[64]{0:T(128)S(1)}, s32[64]{0:T(128)}, u32[]{:S(2)}) copy-start(s32[64]{0:T(128)} %param.15) | copy-start | bytes 772
  62.4 81.1 %all-to-all-start = ((bf16[16,2,128,384]{3,2,1,0:T(8,128)(2,1)}), bf16[16,2,128,384]{3,2,1,0:T(8,128)(2,1)}, u32[]{:S(2)}, u32[]{:S(2)}) async-start(bf16[16,2,128,384]{3,2,1,0:T(8,128)(2,1)} %bitcast.1), calls=%async_computation | async-start | bytes 6291456 | tf_op jit(solution)/shard_map/all_to_all | solution.py:186
  84.3 5.1 %collective-permute-start = (f32[8,128,640]{2,1,0:T(8,128)S(1)}, f32[8,128,640]{2,1,0:T(8,128)}, u32[]{:S(2)}, u32[]{:S(2)}) collective-permute-start(f32[8,128,640]{2,1,0:T(8,128)S(1)} %dynamic-slice_bitcast_fusion), channel_id=1, source_target_pairs={{0,1},{1,0},{2,3},{3,2},{4,5},{5,4},{6,7},{7,6},{8,9},{9,8},{10,11... | collective-permute-start | bytes 7864328 | tf_op jit(solution)/shard_map/ppermute | solution.py:156
  93.5 47.4 %collective-permute-start.1 = (f32[4,128,640]{2,1,0:T(8,128)}, f32[4,128,640]{2,1,0:T(8,128)}, u32[]{:S(2)}, u32[]{:S(2)}) collective-permute-start(f32[4,128,640]{2,1,0:T(8,128)} %dynamic-slice_bitcast_fusion.1), channel_id=1, source_target_pairs={{0,2},{1,3},{2,0},{3,1},{4,6},{5,7},{6,4},{7,5},{8,10},{9,11},{10,... | collective-permute-start | bytes 3932168 | tf_op jit(solution)/shard_map/ppermute | solution.py:156
  94.0 52.9 %copy-start.4 = (s32[256]{0:T(256)S(1)}, s32[256]{0:T(256)}, u32[]{:S(2)}) copy-start(s32[256]{0:T(256)} %param.12) | copy-start | bytes 3076
  94.0 54.7 %copy-start.3 = (s32[256]{0:T(256)S(1)}, s32[256]{0:T(256)}, u32[]{:S(2)}) copy-start(s32[256]{0:T(256)} %param.11) | copy-start | bytes 3076
  143.4 31.3 %all-to-all-start.4 = ((f32[4,128,640]{2,1,0:T(8,128)}), f32[4,128,640]{2,1,0:T(8,128)S(1)}, u32[]{:S(2)}, u32[]{:S(2)}) async-start(f32[4,128,640]{2,1,0:T(8,128)} %bitcast_add_fusion.1), calls=%async_computation.4 | async-start | bytes 2621440 | tf_op jit(solution)/shard_map/all_to_all | solution.py:167
  174.7 1.1 copy-start.2
  175.8 55.5 %all-to-all-start.3 = ((bf16[16,2,128,256]{3,2,1,0:T(8,128)(2,1)}), bf16[16,2,128,256]{3,2,1,0:T(8,128)(2,1)S(1)}, u32[]{:S(2)}, u32[]{:S(2)}) async-start(bf16[16,2,128,256]{3,2,1,0:T(8,128)(2,1)} %bitcast.28), calls=%async_computation.3 | async-start | bytes 4194304 | tf_op jit(solution)/shard_map/all_to_all | solution.py:208
  231.3 1.3 copy-start.1
  232.6 74.7 %all-to-all-start.1 = ((bf16[16,2,128,384]{3,2,1,0:T(8,128)(2,1)}), bf16[16,2,128,384]{3,2,1,0:T(8,128)(2,1)S(1)}, u32[]{:S(2)}, u32[]{:S(2)}) async-start(bf16[16,2,128,384]{3,2,1,0:T(8,128)(2,1)} %bitcast.29), calls=%async_computation.1 | async-start | bytes 6291456 | tf_op jit(solution)/shard_map/all_to_all | solution.py:208
